TPU v7x, 8 devices: a whole 2x2x1 slice. The times are simulated.
8 devices in a mesh: ey: 4 (over z, y, x), ex: 2 (over core).
Axes of the slice: x: 2, y: 2, z: 1, core: 2. Of those that a mesh axis runs over, the one named last changes fastest.
Arguments:
- x: bfloat16 [1024, 2048], P(('ey', 'ex'))
- kv_k: bfloat16 [1024, 512, 1, 128], P(('ey', 'ex'))
- kv_v: bfloat16 [1024, 512, 1, 128], P(('ey', 'ex'))
- lens: int32 [1024], P(('ey', 'ex'))
- topk_idx: int32 [1024, 6], P(('ey', 'ex'))
- gates: float32 [1024, 6], P(('ey', 'ex'))
- ln1: bfloat16 [2048], replicated
- ln2: bfloat16 [2048], replicated
- wq: bfloat16 [2048, 2048], replicated
- wo: bfloat16 [2048, 2048], replicated
- ws1: bfloat16 [2048, 1408], replicated
- ws3: bfloat16 [2048, 1408], replicated
- ws2: bfloat16 [1408, 2048], replicated
- w1: bfloat16 [64, 2048, 1408], P(('ey', 'ex'))
- w3: bfloat16 [64, 2048, 1408], P(('ey', 'ex'))
- w2: bfloat16 [64, 1408, 2048], P(('ey', 'ex'))
Outputs:
- output: bfloat16 [1024, 2048], P(('ey', 'ex'))
All inputs are finite; a program needn't handle non-finite values.
Results may differ from a plain program's by a relative error of at most 0.0124819.
Values are sent between devices in bfloat16 or wider.
A program may use at most 1 GiB of HBM per device.

v0:
```python
import jax
import jax.numpy as jnp
from jax import lax
from jax.sharding import PartitionSpec as P

EPS = 1e-6
BF = jnp.bfloat16
F32 = jnp.float32


def _rms(v, w):
    v = v.astype(F32)
    r = lax.rsqrt(jnp.mean(v * v, axis=-1, keepdims=True) + EPS)
    return (v * r * w.astype(F32)).astype(BF)


def _ffn(u, w1, w3, w2):
    g = jnp.dot(u, w1, preferred_element_type=F32)
    v = jnp.dot(u, w3, preferred_element_type=F32)
    z = (jax.nn.silu(g) * v).astype(BF)
    return jnp.dot(z, w2, preferred_element_type=F32).astype(BF)


def _experts(xin, w1, w3, w2):
    g = jnp.einsum('erd,edf->erf', xin, w1, preferred_element_type=F32)
    v = jnp.einsum('erd,edf->erf', xin, w3, preferred_element_type=F32)
    z = (jax.nn.silu(g) * v).astype(BF)
    return jnp.einsum('erf,efd->erd', z, w2, preferred_element_type=F32).astype(BF)


def _attn(x, kk, vv, lens, ln1, wq, wo):
    b, l, kvh, dh = kk.shape
    hq = wq.shape[1] // dh
    a = _rms(x, ln1)
    q = jnp.dot(a, wq, preferred_element_type=F32).astype(BF).reshape(b, kvh, hq // kvh, dh)
    s = jnp.einsum('bkgd,blkd->bkgl', q, kk, preferred_element_type=F32) * dh ** -0.5
    valid = jnp.arange(l)[None, :] < lens[:, None]
    s = jnp.where(valid[:, None, None, :], s, -jnp.inf)
    p = jax.nn.softmax(s, axis=-1).astype(BF)
    o = jnp.einsum('bkgl,blkd->bkgd', p, vv, preferred_element_type=F32).astype(BF)
    attn = jnp.dot(o.reshape(b, hq * dh), wo, preferred_element_type=F32)
    return (x.astype(F32) + attn).astype(BF)


def _ranks(topk, n_exp):
    chosen = (topk[..., None] == jnp.arange(n_exp)).any(axis=-2).astype(jnp.int32)
    before = jnp.cumsum(chosen, axis=-2) - chosen
    return jnp.take_along_axis(before, topk, axis=-1)


def solution(mesh):
    ey, ex = mesh.shape['ey'], mesh.shape['ex']
    ndev = ey * ex
    rows = P(('ey', 'ex'))
    rep = P()

    def local(x, kv_k, kv_v, lens, topk_idx, gates, ln1, ln2, wq, wo, ws1, ws3, ws2, w1, w3, w2):
        b, d = x.shape
        k = topk_idx.shape[1]
        edev = w1.shape[0]
        n_exp = edev * ndev
        cap = max(4, (2 * b * k + n_exp - 1) // n_exp)
        nslotv = ex * edev * ey * cap
        iy = lax.axis_index('ey')

        h = _attn(x, kv_k, kv_v, lens, ln1, wq, wo)
        u = _rms(h, ln2)

        u_g = lax.all_gather(u, 'ey')
        t_g = lax.all_gather(topk_idx, 'ey')
        g_g = lax.all_gather(gates, 'ey')

        rank = _ranks(t_g, n_exp)
        mine = (t_g // (edev * ex) == iy) & (rank < cap)
        src = jnp.arange(ey, dtype=jnp.int32)[:, None, None]
        dest = ((t_g // edev) % ex) * edev + t_g % edev
        pos = jnp.where(mine, (dest * ey + src) * cap + rank, nslotv).reshape(-1)
        tok = jnp.broadcast_to(jnp.arange(ey * b, dtype=jnp.int32).reshape(ey, b, 1), t_g.shape).reshape(-1)
        slot_tok = jnp.full((nslotv,), ey * b, jnp.int32).at[pos].set(tok, mode='drop')
        slot_gate = jnp.zeros((nslotv,), F32).at[pos].set(g_g.reshape(-1), mode='drop')
        u_pad = jnp.concatenate([u_g.reshape(ey * b, d), jnp.zeros((1, d), BF)], axis=0)

        send = u_pad[slot_tok].reshape(ex, edev, ey * cap, d)
        recv = lax.all_to_all(send, 'ex', 0, 0)
        xin = recv.transpose(1, 0, 2, 3).reshape(edev, ex * ey * cap, d)
        out = _experts(xin, w1, w3, w2)
        back = out.reshape(edev, ex, ey * cap, d).transpose(1, 0, 2, 3)
        ret = lax.all_to_all(back, 'ex', 0, 0).reshape(nslotv, d)

        partial = jnp.zeros((ey * b + 1, d), F32).at[slot_tok].add(slot_gate[:, None] * ret.astype(F32))
        routed = lax.psum_scatter(partial[: ey * b].reshape(ey, b, d), 'ey', scatter_dimension=0)
        y = h.astype(F32) + _ffn(u, ws1, ws3, ws2).astype(F32) + routed
        return y.astype(BF)

    return jax.shard_map(
        local, mesh=mesh,
        in_specs=(rows, rows, rows, rows, rows, rows, rep, rep, rep, rep, rep, rep, rep, rows, rows, rows),
        out_specs=rows, check_vma=False)
```

profile of v0, /device:TPU:0, one launch (start us, length us, event | category | flops | bytes accessed | tf_op | source)
XLA Modules:
  0.0 301.9 jit_solution(8462989902303214218)
XLA Ops:
  6.5 0.7 convert_element_type.62
  7.2 1.2 fusion.27
  8.5 4.9 %fusion.26 = bf16[16,8,16,128]{3,1,2,0:T(8,128)(2,1)S(1)} fusion(bf16[2048,2048]{1,0:T(8,128)(2,1)} %param.24, bf16[128,2048]{1,0:T(8,128)(2,1)} %param.16, f32[2048]{0:T(1024)S(1)} %convert_element_type.62, f32[128]{0:T(128)S(1)} %add_rsqrt_fusion.1), kind=kOutput, calls=%fused_computation.41 | convolution fusion | flops 1075052544 | bytes 9445888 | tf_op jit(solution)/shard_map/dot_general | solution.py:35
  13.4 0.1 copy.34
  13.5 0.1 iota_compare_fusion.1
  13.6 12.2 %fusion.3 = f32[128,16,512]{2,1,0:T(8,128)} fusion(bf16[128,16,128]{2,1,0:T(8,128)(2,1)S(1)} %bitcast.72, bf16[128,512,1,128]{3,1,2,0:T(8,128)(2,1)} %param.17), kind=kOutput, calls=%fused_computation.8 | convolution fusion | flops 268435456 | bytes 21495808 | tf_op jit(solution)/shard_map/bkgd,blkd->bkgl/dot_general | solution.py:36
  25.8 5.4 %fusion.58 = (f32[128,16]{1,0:T(8,128)S(1)}, f32[128,16,512]{2,1,0:T(8,128)S(1)}) fusion(f32[128,16,512]{2,1,0:T(8,128)} %fusion.3, pred[128,512]{1,0:T(8,128)(4,1)S(1)} %iota_compare_fusion.1), kind=kOutput, calls=%fused_computation.97 | output fusion | flops 6291967 | bytes 8462336 | tf_op jit(solution)/shard_map/sub | solution.py:39
  31.2 7.3 %fusion.23 = bf16[128,16,128]{2,1,0:T(8,128)(2,1)S(1)} fusion(bf16[128,512,1,128]{3,1,2,0:T(8,128)(2,1)} %param.18, f32[128,16,512]{2,1,0:T(8,128)S(1)} %get-tuple-element.6, f32[128,16]{1,0:T(8,128)S(1)} %get-tuple-element.5), kind=kOutput, calls=%fused_computation.40 | convolution fusion | flops 270794752 | bytes 21504000 | tf_op jit(solution)/shard_map/bkgl,blkd->bkgd/dot_general | solution.py:40
  38.6 1.5 multiply_reduce_fusion
  40.2 1.0 copy-done
  41.1 1.0 multiply_convert_fusion.1
  42.1 0.0 all-gather.5.cloned.1.call-update
  42.1 0.0 reduce-scatter.4.cloned.1.call-start
  42.2 10.0 %all-gather = s32[512,6]{0,1:T(8,128)S(1)} all-gather(s32[128,6]{0,1:T(8,128)S(1)} %copy-done.5), channel_id=2, replica_groups=mesh['ey'=4,'ex'=2] {'ey'}, dimensions={0}, use_global_device_ids=true | all-gather | bytes 15360 | tf_op jit(solution)/shard_map/all_gather | solution.py:70
  52.2 0.1 copy.28
  52.3 0.1 copy.29
  52.4 0.2 fusion.30
  52.6 0.2 copy.30
  52.8 0.1 bitcast_or_fusion
  52.9 0.2 reshape.181
  53.1 0.3 reduce_window_sum.11
  53.4 25.9 %gather_fusion.1 = s32[3072]{0:T(1024)S(1)} fusion(s32[4,128,64]{2,1,0:T(8,128)S(1)} %convert_subtract_fusion, s32[3072]{0:T(1024)S(1)} %reshape.181), kind=kCustom, calls=%fused_computation.1 | custom fusion | bytes 61440 | tf_op jit(solution)/shard_map/jit(take_along_axis)/gather | solution.py:48
  79.3 0.2 reshape.184
  79.5 0.6 fusion.46
  80.0 0.2 reshape.161
  80.2 0.1 broadcast_in_dim.60
  80.4 0.2 reshape.191
  80.6 8.6 %all-gather.1 = f32[512,6]{0,1:T(8,128)S(1)} all-gather(f32[128,6]{0,1:T(8,128)S(1)} %copy-done.6), channel_id=3, replica_groups=mesh['ey'=4,'ex'=2] {'ey'}, dimensions={0}, use_global_device_ids=true | all-gather | bytes 15360 | tf_op jit(solution)/shard_map/all_gather | solution.py:71
  89.1 0.1 copy.31
  89.3 0.2 reshape.199
  89.5 11.8 %scatter_custom_fusion = s32[1536]{0:T(1024)S(1)} fusion(s32[3072]{0:T(1024)S(1)} %bitcast.74, s32[3072]{0:T(1024)S(1)} %reshape.191, s32[]{:T(128)} %constant.91.clone.1), kind=kCustom, calls=%fused_computation.88 | custom fusion | bytes 6148 | tf_op jit(solution)/shard_map/scatter | solution.py:79
  101.2 11.8 %scatter_custom_fusion.1 = f32[1536]{0:T(1024)S(1)} fusion(s32[3072]{0:T(1024)S(1)} %bitcast.75, f32[3072]{0:T(1024)S(1)} %reshape.199, f32[]{:T(128)} %constant.85.clone.1), kind=kCustom, calls=%fused_computation.86 | custom fusion | bytes 6148 | tf_op jit(solution)/shard_map/scatter | solution.py:80
  113.1 0.0 all-gather.5.cloned.1.call-done
  113.1 1.7 concatenate.3
  114.8 7.1 %gather_fusion = bf16[1536,2048]{1,0:T(8,128)(2,1)} fusion(bf16[513,2048]{1,0:T(8,128)(2,1)S(1)} %concatenate.3, s32[2048]{0:T(1024)S(1)} %pad_clamp_fusion), kind=kCustom, calls=%fused_computation | custom fusion | bytes 12589056 | tf_op jit(solution)/shard_map/gather | solution.py:83
  121.9 10.1 %all_to_all.10 = bf16[2,8,96,2048]{3,2,1,0:T(8,128)(2,1)S(1)} all-to-all(bf16[2,8,96,2048]{3,2,1,0:T(8,128)(2,1)} %bitcast.62), channel_id=1, replica_groups=mesh['ey'=4,'ex'=2] {'ex'}, dimensions={0} | all-to-all | bytes 12582912 | tf_op jit(solution)/shard_map/all_to_all | solution.py:84
  132.1 3.3 %copy.32 = bf16[8,2,96,2048]{3,2,1,0:T(8,128)(2,1)} copy(bf16[8,2,96,2048]{3,2,0,1:T(8,128)(2,1)S(1)} %bitcast.60) | data formatting | bytes 12582912 | tf_op jit(solution)/shard_map/transpose | solution.py:85
  135.3 22.2 %fusion.60 = f32[8,192,1408]{2,1,0:T(8,128)} fusion(bf16[8,192,2048]{2,1,0:T(8,128)(2,1)} %bitcast.66, bf16[8,2048,1408]{2,1,0:T(8,128)(2,1)} %param.29), kind=kOutput, calls=%fused_computation.99 | convolution fusion | flops 8858370048 | bytes 61079552 | tf_op jit(solution)/shard_map/erd,edf->erf/dot_general | solution.py:25
  157.6 25.0 %multiply_convert_fusion.clone.6 = bf16[8,192,1408]{2,1,0:T(8,128)(2,1)} fusion(f32[8,192,1408]{2,1,0:T(8,128)} %fusion.60, bf16[8,192,2048]{2,1,0:T(8,128)(2,1)} %bitcast.67, bf16[8,2048,1408]{2,1,0:T(8,128)(2,1)} %param.30), kind=kOutput, calls=%fused_computation.12.clone.clone.clone.clone.clone.1 | convolution fusion | flops 8871346176 | bytes 65404928 | tf_op jit(solution)/shard_map/erd,edf->erf/dot_general | solution.py:26
  182.6 18.7 %fusion.8 = bf16[8,192,2048]{2,1,0:T(8,128)(2,1)S(1)} fusion(bf16[8,1408,2048]{2,1,0:T(8,128)(2,1)} %param.31, bf16[8,192,1408]{2,1,0:T(8,128)(2,1)} %multiply_convert_fusion.clone.6), kind=kOutput, calls=%fused_computation.16 | convolution fusion | flops 8861515776 | bytes 56754176 | tf_op jit(solution)/shard_map/erf,efd->erd/dot_general | solution.py:28
  201.3 1.1 copy.43
  202.4 9.9 %all_to_all.11 = bf16[2,8,96,2048]{3,2,1,0:T(8,128)(2,1)} all-to-all(bf16[2,8,96,2048]{3,2,1,0:T(8,128)(2,1)S(1)} %bitcast.61), channel_id=1, replica_groups=mesh['ey'=4,'ex'=2] {'ex'}, dimensions={0} | all-to-all | bytes 12582912 | tf_op jit(solution)/shard_map/all_to_all | solution.py:88
  212.3 23.8 %scatter_custom_fusion.2 = f32[513,2048]{1,0:T(8,128)} fusion(s32[1536]{0:T(1024)S(1)} %compare_select_fusion.1, bf16[1536,2048]{1,0:T(8,128)(2,1)} %bitcast.59, f32[1536]{0:T(1024)S(1)} %scatter_custom_fusion.1, f32[]{:T(128)} %constant.85.clone.1), kind=kCustom, calls=%fused_computation.11 | custom fusion | flops 9437184 | bytes 10502148 | tf_op jit(solution)/shard_map/scatter-add | solution.py:90
  236.0 4.7 %slice.9 = f32[512,2048]{1,0:T(8,128)} slice(f32[513,2048]{1,0:T(8,128)} %scatter_custom_fusion.2), slice={[0:512], [0:2048]} | slice | bytes 8388608 | tf_op jit(solution)/shard_map/slice | solution.py:91
  240.7 0.0 reduce-scatter.4.cloned.1.call-update
  240.7 3.7 %fusion.59 = f32[128,1408]{1,0:T(8,128)S(1)} fusion(bf16[128,2048]{1,0:T(8,128)(2,1)S(1)} %copy-done.2, bf16[2048,1408]{1,0:T(8,128)(2,1)} %param.26), kind=kOutput, calls=%fused_computation.98 | convolution fusion | flops 738197504 | bytes 7012352 | tf_op jit(solution)/shard_map/dot_general | solution.py:18
  244.4 43.2 %reduce-scatter.4.cloned.1.call-done = f32[1,128,2048]{2,1,0:T(8,128)} async-done(((f32[4,128,2048]{2,1,0:T(8,128)}), f32[1,128,2048]{2,1,0:T(8,128)}) %reduce-scatter.4.cloned.1.call-update) | async-done | bytes 1048592
  287.7 7.4 %fusion.17 = bf16[128,2048]{1,0:T(8,128)(2,1)} fusion(f32[128,2048]{1,0:T(8,128)S(1)} %copy-done.1, bf16[1408,2048]{1,0:T(8,128)(2,1)} %param.28, f32[1,128,2048]{2,1,0:T(8,128)} %reduce-scatter.4.cloned.1.call-done, bf16[128,2048]{1,0:T(8,128)(2,1)S(1)} %copy-done.2, bf16[2048,1408]{1,0:T(8,128)(2,1)} %param.27, f32[128,1408]{1,0:T(8,128)S(1)} %fusion.59), kind=kOutput, calls=%fused_computation.32 | convolution fusion | flops 1478787072 | bytes 15400960 | tf_op jit(solution)/shard_map/dot_general | solution.py:21
  (30 shorter events, 0.1 us)
Async XLA Ops:
  6.5 106.6 %all-gather.5.cloned.1.call-start = ((), (), s32[]{:S(2)}) async-start(), calls=%async_computation.3 | async-start | bytes 2621440 | tf_op jit(solution)/shard_map/all_gather | solution.py:69
  8.5 5.0 %copy-start.7 = (s32[128]{0:T(128)S(1)}, s32[128]{0:T(128)}, u32[]{:S(2)}) copy-start(s32[128]{0:T(128)} %param.19) | copy-start | bytes 1540
  25.8 12.8 %slice-start = ((s8[8388608]{0:T(1024)(128)(4,1)}), s8[4194304]{0:T(1024)(128)(4,1)S(1)}, s32[]{:S(2)}) async-start(s8[8388608]{0:T(1024)(128)(4,1)} %bitcast.63), calls=%async_computation.5 | async-start | bytes 8388608
  31.2 7.4 %slice-start.1 = ((s8[8388608]{0:T(1024)(128)(4,1)}), s8[4194304]{0:T(1024)(128)(4,1)S(1)}, s32[]{:S(2)}) async-start(s8[8388608]{0:T(1024)(128)(4,1)} %bitcast.63), calls=%async_computation.6 | async-start | bytes 8388608
  31.2 7.4 %copy-start.3 = (bf16[128,2048]{1,0:T(8,128)(2,1)S(1)}, bf16[128,2048]{1,0:T(8,128)(2,1)}, u32[]{:S(2)}) copy-start(bf16[128,2048]{1,0:T(8,128)(2,1)} %param.16) | copy-start | bytes 1572868
  38.6 1.5 copy-start.4
  38.6 3.5 %copy-start.5 = (s32[128,6]{0,1:T(8,128)S(1)}, s32[128,6]{0,1:T(8,128)}, u32[]{:S(2)}) copy-start(s32[128,6]{0,1:T(8,128)} %param.20) | copy-start | bytes 9220
  40.1 1.0 copy-start
  42.1 245.6 %reduce-scatter.4.cloned.1.call-start = ((), (), s32[]{:S(2)}) async-start(), calls=%async_computation.4 | async-start | bytes 5242880
  53.3 27.2 %copy-start.6 = (f32[128,6]{0,1:T(8,128)S(1)}, f32[128,6]{0,1:T(8,128)}, u32[]{:S(2)}) copy-start(f32[128,6]{0,1:T(8,128)} %param.21) | copy-start | bytes 9220
  236.0 4.7 %copy-start.2 = (bf16[128,2048]{1,0:T(8,128)(2,1)S(1)}, bf16[128,2048]{1,0:T(8,128)(2,1)}, u32[]{:S(2)}) copy-start(bf16[128,2048]{1,0:T(8,128)(2,1)} %multiply_convert_fusion.1) | copy-start | bytes 1572868
  240.7 47.0 %copy-start.1 = (f32[128,2048]{1,0:T(8,128)S(1)}, f32[128,2048]{1,0:T(8,128)}, u32[]{:S(2)}) copy-start(f32[128,2048]{1,0:T(8,128)} %copy-done) | copy-start | bytes 3145732
Sparse Core Ops, SparseCore 0:
  42.2 32.1 all-gather.4
  240.8 46.7 reduce-scatter.3
where the time goes:
time: 302 us
  matrix products  103 us (34%)
  local copies, waits for them, and re-layouts  70 us (23%)
  waiting for transfers between devices  43.3 us (14%)
  blocking collectives  38.5 us (13%)
  other arithmetic  33.3 us (11%)
  between operations  13.8 us (5%)
    unnamed x3, waiting for transfers between devices  43.3 us
    gather x3, local copies, waits for them, and re-layouts, _ranks(): return jnp.take_along_axis(before, topk, axis=-1)  26.3 us
    dot_general x1, matrix products, _experts(): v = jnp.einsum('erd,edf->erf', xin, w3, preferred_element_type=F32)  25 us
    scatter-add x1, other arithmetic, local(): jnp.zeros((ey * b + 1, d), F32).at[slot_tok]  23.8 us
    dot_general x1, matrix products, _experts(): g = jnp.einsum('erd,edf->erf', xin, w1, preferred_element_type=F32)  22.2 us
    dot_general x1, matrix products, _experts(): jnp.einsum('erf,efd->erd', z, w2, preferred_element_type=F32).astype(BF)  18.7 us
    dot_general x1, matrix products, _attn(): jnp.einsum('bkgd,blkd->bkgl', q, kk, preferred_element_type=F32)  12.2 us
    scatter x1, local copies, waits for them, and re-layouts, local(): jnp.full((nslotv,), ey * b, jnp.int32).at[pos].set(tok, mode='drop')  11.8 us
  transfers between devices with their start and end apart: 2, of which 1 were waited for; matrix products, arithmetic and copies ran while one was open for 19% of the time, Pallas kernels for 0%

commit v1 on v0

v1 whole, which is shorter than its diff:
```python
import functools

import jax
import jax.numpy as jnp
from jax import lax
from jax.experimental import pallas as pl
from jax.experimental.pallas import tpu as pltpu
from jax.sharding import PartitionSpec as P

EPS = 1e-6
BF = jnp.bfloat16
F32 = jnp.float32
MESH = pl.DeviceIdType.MESH
NK = 4
N1 = 4
N2 = 6
PIECES = 3


def _rms(v, w):
    v = v.astype(F32)
    r = lax.rsqrt(jnp.mean(v * v, axis=-1, keepdims=True) + EPS)
    return (v * r * w.astype(F32)).astype(BF)


def _attn(x, kk, vv, lens, ln1, wq, wo):
    b, l, kvh, dh = kk.shape
    hq = wq.shape[1] // dh
    a = _rms(x, ln1)
    q = jnp.dot(a, wq, preferred_element_type=F32).astype(BF).reshape(b, kvh, hq // kvh, dh)
    s = jnp.einsum('bkgd,blkd->bkgl', q, kk, preferred_element_type=F32) * dh ** -0.5
    valid = jnp.arange(l)[None, :] < lens[:, None]
    s = jnp.where(valid[:, None, None, :], s, -jnp.inf)
    p = jax.nn.softmax(s, axis=-1).astype(BF)
    o = jnp.einsum('bkgl,blkd->bkgd', p, vv, preferred_element_type=F32).astype(BF)
    attn = jnp.dot(o.reshape(b, hq * dh), wo, preferred_element_type=F32)
    return (x.astype(F32) + attn).astype(BF)


def _tables(topk, gates, n_exp, ndev, cap, ex_idx):
    b = topk.shape[0]
    hit = topk.T[None, :, :] == jnp.arange(n_exp, dtype=topk.dtype)[:, None, None]
    chosen = hit.any(axis=1)
    gate = jnp.where(hit, gates.T[None, :, :], 0.0).sum(axis=1)
    tri = (jnp.arange(b)[:, None] < jnp.arange(b)[None, :]).astype(BF)
    before = jnp.dot(chosen.astype(BF), tri, preferred_element_type=F32)
    slot = jnp.where(chosen & (before < cap), before + (cap * ex_idx).astype(F32), -1.0)
    return jnp.stack([slot.reshape(ndev, -1, b), gate.reshape(ndev, -1, b)], axis=1)


def _moe_kernel(dims, u_ref, h_ref, tab_ref, w1, w3, w2, ws1, ws3, ws2, y_ref,
                uall, tabs, sel, wgt, xin, acc, z, zs, sh, outb, d2d, rx1, rx2, r13, r2,
                s13, sw2, tsend, trecv, usend, urecv, uloc, dsend, drecv, psend, precv, qsend, qrecv):
    b, d, ff, el, cap = dims
    cw = d // NK
    pair = 2 * cap
    rows = 4 * pair
    ey = lax.axis_index('ey')
    ex = lax.axis_index('ex')
    me = ey * 2 + ex
    ox = 1 - ex
    cx, cy = ey % 2, ey // 2
    xn = cy * 2 + (1 - cx)
    yn = (1 - cy) * 2 + cx
    dg = (1 - cy) * 2 + (1 - cx)
    partner, xdev, ydev = (ey, ox), (xn, ex), (yn, ex)

    n13 = NK + NK * el
    n2 = NK * (el + 1)

    def cp13(src, slot, i):
        return pltpu.make_async_copy(src, r13.at[slot, i], s13.at[slot, i])

    def start13(s):
        slot = s % N1

        @pl.when(s < NK)
        def _():
            ks = pl.ds(pl.multiple_of(s * cw, cw), cw)
            cp13(ws1.at[ks, :], slot, 0).start()
            cp13(ws3.at[ks, :], slot, 1).start()

        @pl.when(s >= NK)
        def _():
            t = s - NK
            e = t % el
            ks = pl.ds(pl.multiple_of((t // el) * cw, cw), cw)
            cp13(w1.at[e, ks, :], slot, 0).start()
            cp13(w3.at[e, ks, :], slot, 1).start()

    def wait13(s):
        slot = s % N1
        for i in range(2):
            cp13(w1.at[0, pl.ds(0, cw), :], slot, i).wait()

    def start2(j):
        slot = j % N2
        c = j // (el + 1)
        i = j % (el + 1)
        cs = pl.ds(pl.multiple_of(c * cw, cw), cw)

        @pl.when(i < el)
        def _():
            pltpu.make_async_copy(w2.at[i, :, cs], r2.at[slot], sw2.at[slot]).start()

        @pl.when(i == el)
        def _():
            pltpu.make_async_copy(ws2.at[:, cs], r2.at[slot], sw2.at[slot]).start()

    def wait2(j):
        slot = j % N2
        pltpu.make_async_copy(w2.at[0, :, pl.ds(0, cw)], r2.at[slot], sw2.at[slot]).wait()

    for s in range(N1):
        start13(jnp.int32(s))

    barrier = pltpu.get_barrier_semaphore()
    for o in range(1, 8):
        peer = (me + o) % 8
        pl.semaphore_signal(barrier, inc=1, device_id=(peer // 2, peer % 2), device_id_type=MESH)
    pl.semaphore_wait(barrier, 7)

    def ublk(k, chip, e):
        return uall.at[k, chip, pl.ds(pl.multiple_of(e * b, b), b), :]

    def ucopy(k, i, src, chip, e, role, dev):
        return pltpu.make_async_remote_copy(
            src_ref=src, dst_ref=ublk(k, chip, e), send_sem=usend.at[k, i], recv_sem=urecv.at[k, role],
            device_id=dev, device_id_type=MESH)

    def uown(k):
        return u_ref.at[:, pl.ds(k * cw, cw)]

    def direct(k):
        cps = [ucopy(k, 1, uown(k), ey, ex, 1, xdev), ucopy(k, 2, uown(k), ey, ex, 2, ydev),
               ucopy(k, 0, uown(k), ey, ex, 0, partner)]
        for cp in cps:
            cp.start()
        pltpu.make_async_copy(uown(k), ublk(k, ey, ex), uloc.at[k]).start()

    def urcv(k, role, chip, e):
        return ucopy(k, 0, uown(k), chip, e, role, partner)

    def forward(k):
        urcv(k, 1, xn, ex).wait_recv()
        if k % 2 == 0:
            ucopy(k, 3, ublk(k, xn, ex), xn, ex, 3, ydev).start()
        ucopy(k, 4, ublk(k, xn, ex), xn, ex, 4, partner).start()
        urcv(k, 2, yn, ex).wait_recv()
        if k % 2 == 1:
            ucopy(k, 3, ublk(k, yn, ex), yn, ex, 3, xdev).start()
        ucopy(k, 5, ublk(k, yn, ex), yn, ex, 5, partner).start()

    def forward_diag(k):
        urcv(k, 3, dg, ex).wait_recv()
        ucopy(k, 6, ublk(k, dg, ex), dg, ex, 6, partner).start()

    def arrived(k):
        pltpu.make_async_copy(uown(k), ublk(k, ey, ex), uloc.at[k]).wait()
        urcv(k, 0, ey, ox).wait_recv()
        urcv(k, 4, xn, ox).wait_recv()
        urcv(k, 5, yn, ox).wait_recv()
        urcv(k, 6, dg, ox).wait_recv()

    direct(0)

    def tcopy(o, peer):
        return pltpu.make_async_remote_copy(
            src_ref=tab_ref.at[peer], dst_ref=tabs.at[me], send_sem=tsend.at[o - 1], recv_sem=trecv.at[o - 1],
            device_id=(peer // 2, peer % 2), device_id_type=MESH)

    for o in range(1, 8):
        tcopy(o, (me + o) % 8).start()
    tabs[me] = tab_ref[me]
    direct(1)

    def silu_mul(g, v):
        return (g * (1.0 / (1.0 + jnp.exp(-g))) * v).astype(BF)

    nts = [(n, min(512, ff - n)) for n in range(0, ff, 512)]

    for s in range(NK):
        wait13(s)
        for n, nw in nts:
            for i in range(2):
                p = jnp.dot(u_ref[:, s * cw:(s + 1) * cw], r13[s % N1, i, :, n:n + nw], preferred_element_type=F32)
                if s > 0:
                    p = acc[i, 0:b, n:n + nw] + p
                acc[i, 0:b, n:n + nw] = p
        start13(jnp.int32(s + N1))
    for n, nw in nts:
        zs[:, n:n + nw] = silu_mul(acc[0, 0:b, n:n + nw], acc[1, 0:b, n:n + nw])

    for o in range(1, 8):
        src = (me + 8 - o) % 8
        pltpu.make_async_remote_copy(
            src_ref=tab_ref.at[src], dst_ref=tabs.at[src], send_sem=tsend.at[o - 1], recv_sem=trecv.at[o - 1],
            device_id=(src // 2, src % 2), device_id_type=MESH).wait_recv()
    iota = lax.broadcasted_iota(jnp.int32, (pair, 2 * b), 0).astype(F32)

    def build(c, _):
        t = jnp.concatenate([tabs[2 * c, 0], tabs[2 * c + 1, 0]], axis=1)
        g = jnp.concatenate([tabs[2 * c, 1], tabs[2 * c + 1, 1]], axis=1)
        one = []
        gat = []
        for e in range(el):
            m = iota == t[e:e + 1, :]
            one.append(jnp.where(m, 1.0, 0.0))
            gat.append(jnp.where(m, g[e:e + 1, :], 0.0))
        sel[c] = jnp.concatenate(one, axis=0).astype(BF)
        gt = jnp.concatenate(gat, axis=0).T
        for i in range(PIECES):
            piece = gt.astype(BF)
            wgt[i, c] = piece
            gt = gt - piece.astype(F32)
        return 0

    lax.fori_loop(0, 4, build, 0)

    forward(0)
    direct(2)
    forward_diag(0)

    for k in range(NK):
        arrived(k)

        def pick(c, _, k=k):
            r = jnp.dot(sel[c], uall[k, c], preferred_element_type=F32).astype(BF)
            for e in range(el):
                xin[e, pl.ds(pl.multiple_of(c * pair, pair), pair), :] = r[e * pair:(e + 1) * pair, :]
            return 0

        lax.fori_loop(0, 4, pick, 0)

        def zstep(e, _, k=k):
            s = NK + k * el + e
            wait13(s)
            slot = s % N1
            er = pl.ds(pl.multiple_of(e * rows, rows), rows)
            for n, nw in nts:
                ps = []
                for i in range(2):
                    p = jnp.dot(xin[e], r13[slot, i, :, n:n + nw], preferred_element_type=F32)
                    if k > 0:
                        p = acc[i, er, n:n + nw] + p
                    ps.append(p)
                if k < NK - 1:
                    acc[0, er, n:n + nw] = ps[0]
                    acc[1, er, n:n + nw] = ps[1]
                else:
                    z[e, :, n:n + nw] = silu_mul(ps[0], ps[1])
            nxt = s + N1

            @pl.when(nxt < n13)
            def _():
                start13(nxt)

            if k == NK - 1:
                @pl.when(nxt >= n13)
                def _():
                    start2(nxt - n13)
            return 0

        half = el // 2
        lax.fori_loop(0, half, zstep, 0)
        if k + 1 < NK:
            forward(k + 1)
            if k + 3 < NK:
                direct(k + 3)
        lax.fori_loop(half, el, zstep, 0)
        if k + 1 < NK:
            forward_diag(k + 1)
    for j in range(N1, N2):
        start2(jnp.int32(j))

    def part(c, e, chip):
        return acc.at[c // 2, pl.ds(pl.multiple_of((e * 4 + chip) * b, b), b), pl.ds((c % 2) * cw, cw)]

    def nbr(c):
        return (xn, xdev, yn, ydev) if c % 2 == 0 else (yn, ydev, xn, xdev)

    def dcopy(c):
        src = acc.at[c // 2, pl.ds(pl.multiple_of(ox * 4 * b, 4 * b), 4 * b), pl.ds((c % 2) * cw, cw)]
        return pltpu.make_async_remote_copy(
            src_ref=src, dst_ref=d2d.at[c], send_sem=dsend.at[c], recv_sem=drecv.at[c],
            device_id=partner, device_id_type=MESH)

    def pcopy(c, i):
        n1, dev1, n2_, dev2 = nbr(c)
        return pltpu.make_async_remote_copy(
            src_ref=part(c, ex, n1 if i == 0 else dg), dst_ref=rx1.at[c, i], send_sem=psend.at[c, i],
            recv_sem=precv.at[c, i], device_id=dev1, device_id_type=MESH)

    def qcopy(c):
        n1, dev1, n2_, dev2 = nbr(c)
        return pltpu.make_async_remote_copy(
            src_ref=part(c, ex, n2_), dst_ref=rx2.at[c], send_sem=qsend.at[c], recv_sem=qrecv.at[c],
            device_id=dev2, device_id_type=MESH)

    def step_a(c):
        def down(e, _):
            j = c * (el + 1) + e
            wait2(j)
            r = jnp.dot(z[e], r2[j % N2], preferred_element_type=F32).astype(BF)
            for q in range(4):
                outb[q, pl.ds(pl.multiple_of(e * pair, pair), pair), :] = r[q * pair:(q + 1) * pair, :]

            @pl.when(j + N2 < n2)
            def _():
                start2(j + N2)
            return 0

        lax.fori_loop(0, el, down, 0)

        def comb(q, _):
            p = jnp.dot(wgt[0, q], outb[q], preferred_element_type=F32)
            for i in range(1, PIECES):
                p = p + jnp.dot(wgt[i, q], outb[q], preferred_element_type=F32)
            part(c, 0, q)[...] = p[0:b]
            part(c, 1, q)[...] = p[b:2 * b]
            return 0

        lax.fori_loop(0, 4, comb, 0)
        dcopy(c).start()
        j = c * (el + 1) + el
        wait2(jnp.int32(j))
        sh[:, c * cw:(c + 1) * cw] = jnp.dot(zs[...], r2[j % N2], preferred_element_type=F32).astype(BF)
        if j + N2 < n2:
            start2(jnp.int32(j + N2))

    def step_b(c):
        dcopy(c).wait_recv()

        def add(q, _):
            part(c, ex, q)[...] = part(c, ex, q)[...] + d2d[c, pl.ds(pl.multiple_of(q * b, b), b), :]
            return 0

        lax.fori_loop(0, 4, add, 0)
        pcopy(c, 1).start()
        pcopy(c, 0).start()

    def step_c(c):
        n1, dev1, n2_, dev2 = nbr(c)
        pcopy(c, 1).wait_recv()
        pcopy(c, 1).wait_send()
        part(c, ex, n2_)[...] = part(c, ex, n2_)[...] + rx1[c, 1]
        qcopy(c).start()

    def step_d(c):
        pcopy(c, 0).wait_recv()
        qcopy(c).wait_recv()
        cs = slice(c * cw, (c + 1) * cw)
        t = part(c, ex, ey)[...] + rx1[c, 0] + rx2[c]
        y_ref[:, cs] = (h_ref[:, cs].astype(F32) + sh[:, cs].astype(F32) + t).astype(BF)

    step_a(0)
    step_a(1)
    step_b(0)
    step_b(1)
    step_a(2)
    step_c(0)
    step_c(1)
    step_a(3)
    step_b(2)
    step_b(3)
    step_d(0)
    step_d(1)
    step_c(2)
    step_c(3)
    step_d(2)
    step_d(3)

    for o in range(1, 8):
        tcopy(o, (me + o) % 8).wait_send()
    for k in range(NK):
        for i in range(7):
            ucopy(k, i, uown(k), ey, ex, 0, partner).wait_send()
    for c in range(NK):
        dcopy(c).wait_send()
        pcopy(c, 0).wait_send()
        qcopy(c).wait_send()


def _moe(u, h, tab, w1, w3, w2, ws1, ws3, ws2, cap):
    b, d = u.shape
    el, _, ff = w1.shape
    ndev, _, _, _ = tab.shape
    cw = d // NK
    pair = 2 * cap
    rows = 4 * pair
    vm = pl.BlockSpec(memory_space=pltpu.VMEM)
    hb = pl.BlockSpec(memory_space=pltpu.HBM)
    dma = pltpu.SemaphoreType.DMA
    return pl.pallas_call(
        functools.partial(_moe_kernel, (b, d, ff, el, cap)),
        out_shape=jax.ShapeDtypeStruct((b, d), BF),
        in_specs=[vm, vm, vm, hb, hb, hb, hb, hb, hb],
        out_specs=vm,
        scratch_shapes=[
            pltpu.VMEM((NK, 4, 2 * b, cw), BF),
            pltpu.VMEM((ndev, 2, el, b), F32),
            pltpu.VMEM((4, el * pair, 2 * b), BF),
            pltpu.VMEM((PIECES, 4, 2 * b, el * pair), BF),
            pltpu.VMEM((el, rows, cw), BF),
            pltpu.VMEM((2, el * rows, ff), F32),
            pltpu.VMEM((el, rows, ff), BF),
            pltpu.VMEM((b, ff), BF),
            pltpu.VMEM((b, d), BF),
            pltpu.VMEM((4, el * pair, cw), BF),
            pltpu.VMEM((NK, 4 * b, cw), F32),
            pltpu.VMEM((NK, 2, b, cw), F32),
            pltpu.VMEM((NK, b, cw), F32),
            pltpu.VMEM((N1, 2, cw, ff), BF),
            pltpu.VMEM((N2, ff, cw), BF),
            dma((N1, 2)), dma((N2,)),
            dma((7,)), dma((7,)),
            dma((NK, 7)), dma((NK, 7)), dma((NK,)),
            dma((NK,)), dma((NK,)),
            dma((NK, 2)), dma((NK, 2)),
            dma((NK,)), dma((NK,)),
        ],
        compiler_params=pltpu.CompilerParams(
            collective_id=0, has_side_effects=True, vmem_limit_bytes=67043328),
        name='moe',
    )(u, h, tab, w1, w3, w2, ws1, ws3, ws2)


def solution(mesh):
    ey, ex = mesh.shape['ey'], mesh.shape['ex']
    ndev = ey * ex
    rows = P(('ey', 'ex'))
    rep = P()

    def local(x, kv_k, kv_v, lens, topk_idx, gates, ln1, ln2, wq, wo, ws1, ws3, ws2, w1, w3, w2):
        b = x.shape[0]
        n_exp = w1.shape[0] * ndev
        cap = max(4, (2 * b * topk_idx.shape[1] + n_exp - 1) // n_exp)
        tab = _tables(topk_idx, gates, n_exp, ndev, cap, lax.axis_index('ex'))
        h = _attn(x, kv_k, kv_v, lens, ln1, wq, wo)
        u = _rms(h, ln2)
        return _moe(u, h, tab, w1, w3, w2, ws1, ws3, ws2, cap)

    return jax.shard_map(
        local, mesh=mesh,
        in_specs=(rows, rows, rows, rows, rows, rows, rep, rep, rep, rep, rep, rep, rep, rows, rows, rows),
        out_specs=rows, check_vma=False)
```

time: 302 us -> 147 us (0.49)
  Pallas kernels: 0 us -> 108 us
  matrix products: 103 us -> 26.3 us
  local copies, waits for them, and re-layouts: 70 us -> 2.8 us
  waiting for transfers between devices: 43.3 us -> 0 us
  blocking collectives: 38.5 us -> 0 us
  other arithmetic: 33.3 us -> 9.1 us
  between operations: 13.8 us -> 0.19 us
    pallas_call x0 -> x1, Pallas kernels: none -> 108 us  [_moe(): pl.pallas_call(functools.partial(_moe_kernel, (b, d, ff, el, cap)), out_s...]
    dot_general x5 -> x1, matrix products: 77 us -> 0.14 us  [_tables(): before = jnp.dot(chosen.astype(BF), tri, preferred_element_type=F32)]
    unnamed x3 -> x0, waiting for transfers between devices: 43.3 us -> none
    gather x4 -> x0, local copies, waits for them, and re-layouts: 33.4 us -> none  [the longest x3 26.3 us: _ranks(): return jnp.take_along_axis(before, topk, axis=-1)]
    scatter-add x1 -> x0, other arithmetic: 23.8 us -> none  [local(): jnp.zeros((ey * b + 1, d), F32).at[slot_tok]]
    scatter x2 -> x0, local copies, waits for them, and re-layouts: 23.6 us -> none  [the longest x1 11.8 us: local(): jnp.full((nslotv,), ey * b, jnp.int32).at[pos].set(tok, mode='drop')]
    all_to_all x2 -> x0, blocking collectives: 20 us -> none  [the longest x1 10.1 us: local(): recv = lax.all_to_all(send, 'ex', 0, 0)]
    all_gather x2 -> x0, blocking collectives: 18.6 us -> none  [the longest x1 10 us: local(): t_g = lax.all_gather(topk_idx, 'ey')]
  transfers between devices with their start and end apart: 2 -> 0, of which waited for: 1 -> 0; matrix products, arithmetic and copies ran while one was open for 19% -> 0% of each run, Pallas kernels for 0% -> 0%
where the time goes in v1:
time: 147 us
  Pallas kernels  108 us (73%)
  matrix products  26.3 us (18%)
  other arithmetic  9.1 us (6%)
  local copies, waits for them, and re-layouts  2.8 us (2%)
    pallas_call x1, Pallas kernels, _moe(): pl.pallas_call(functools.partial(_moe_kernel, (b, d, ff, el, cap)), out_s...  108 us
    dot_general x1, matrix products, _attn(): jnp.einsum('bkgd,blkd->bkgl', q, kk, preferred_element_type=F32)  12.2 us
    dot_general x1, matrix products, _attn(): jnp.einsum('bkgl,blkd->bkgd', p, vv, preferred_element_type=F32).astype(BF)  7.51 us
    sub x1, other arithmetic, _attn(): p = jax.nn.softmax(s, axis=-1).astype(BF)  5.41 us
    dot_general x1, matrix products, _attn(): jnp.dot(a, wq, preferred_element_type=F32).astype(BF)  4.89 us

profile of v1, /device:TPU:0, one launch (start us, length us, event | category | flops | bytes accessed | tf_op | source)
XLA Modules:
  0.0 146.7 jit_solution(3682863932865754725)
XLA Ops:
  0.0 0.7 convert_element_type.39
  0.7 1.2 fusion.18
  1.9 4.9 %fusion.14 = bf16[16,8,16,128]{3,1,2,0:T(8,128)(2,1)S(1)} fusion(bf16[2048,2048]{1,0:T(8,128)(2,1)} %param.24, bf16[128,2048]{1,0:T(8,128)(2,1)} %param.16, f32[2048]{0:T(1024)S(1)} %convert_element_type.39, f32[128]{0:T(128)S(1)} %add_rsqrt_fusion.1), kind=kOutput, calls=%fused_computation.21 | convolution fusion | flops 1075052544 | bytes 9445888 | tf_op jit(solution)/shard_map/dot_general | solution.py:30
  6.8 0.1 copy.17
  7.0 0.0 copy-start.5
  7.0 12.2 %fusion.3 = f32[128,16,512]{2,1,0:T(8,128)} fusion(bf16[128,16,128]{2,1,0:T(8,128)(2,1)S(1)} %bitcast.28, bf16[128,512,1,128]{3,1,2,0:T(8,128)(2,1)} %param.17), kind=kOutput, calls=%fused_computation.3 | convolution fusion | flops 268435456 | bytes 21495808 | tf_op jit(solution)/shard_map/bkgd,blkd->bkgl/dot_general | solution.py:31
  19.1 0.0 copy-done.5
  19.1 0.1 iota_compare_fusion
  19.3 0.0 slice-start
  19.3 5.4 %fusion.30 = (f32[128,16]{1,0:T(8,128)S(1)}, f32[128,16,512]{2,1,0:T(8,128)S(1)}) fusion(f32[128,16,512]{2,1,0:T(8,128)} %fusion.3, pred[128,512]{1,0:T(8,128)(4,1)S(1)} %iota_compare_fusion), kind=kOutput, calls=%fused_computation.44 | output fusion | flops 6291967 | bytes 8462336 | tf_op jit(solution)/shard_map/sub | solution.py:34
  24.7 0.0 slice-start.1
  24.7 0.0 copy-start
  24.7 7.5 %fusion.11 = bf16[128,16,128]{2,1,0:T(8,128)(2,1)S(1)} fusion(bf16[128,512,1,128]{3,1,2,0:T(8,128)(2,1)} %param.18, f32[128,16,512]{2,1,0:T(8,128)S(1)} %get-tuple-element.6, f32[128,16]{1,0:T(8,128)S(1)} %get-tuple-element.5), kind=kOutput, calls=%fused_computation.20 | convolution fusion | flops 270794752 | bytes 21504000 | tf_op jit(solution)/shard_map/bkgl,blkd->bkgd/dot_general | solution.py:35
  32.2 0.0 slice-done
  32.2 0.0 slice-done.1
  32.2 0.0 copy-done
  32.3 0.0 copy-start.3
  32.3 0.0 copy-start.2
  32.3 0.0 copy-start.4
  32.3 1.5 %fusion.15 = (f32[128]{0:T(128)S(1)}, bf16[128,2048]{1,0:T(8,128)(2,1)S(1)}) fusion(bf16[2048,2048]{1,0:T(8,128)(2,1)S(1)} %bitcast.27, bf16[16,8,16,128]{3,2,1,0:T(8,128)(2,1)S(1)} %bitcast.29, bf16[128,2048]{1,0:T(8,128)(2,1)S(1)} %copy-done), kind=kOutput, calls=%fused_computation.22 | convolution fusion | flops 1075314560 | bytes 9961984 | tf_op jit(solution)/shard_map/dot_general | solution.py:36
  33.8 0.0 copy-start.1
  33.9 0.0 copy-done.3
  33.9 0.8 copy-done.1
  34.6 1.0 fusion.17.u_ref
  35.6 0.0 copy-done.2
  35.6 0.1 select_bitcast_fusion
  35.8 0.0 copy-done.4
  35.8 0.6 pad_maximum_fusion.tab_ref
  36.5 108.3 %moe.1 = bf16[128,2048]{1,0:T(8,128)(2,1)} custom-call(bf16[128,2048]{1,0:T(8,128)(2,1)} %fusion.17.u_ref, bf16[128,2048]{1,0:T(8,128)(2,1)} %copy-done.1, f32[8,2,8,128]{3,2,1,0:T(8,128)} %pad_maximum_fusion.tab_ref, bf16[8,2048,1408]{2,1,0:T(8,128)(2,1)} %w1.1, bf16[8,2048,1408]{2,1,0:T(8,128)(2,1)} %w3.1, bf16[8,1408,2048]{2,1,0:T(8,128)(2,1)} %w2.1, ...), custom_call_target="tpu_custom_call" | custom-call | tf_op jit(solution)/shard_map/moe/pallas_call | solution.py:394
  144.8 1.9 %copy.26 = bf16[128,2048]{1,0:T(8,128)(2,1)} copy(bf16[128,2048]{1,0:T(8,128)(2,1)} %moe.1) | data formatting | bytes 1048576
  (6 shorter events, 0.1 us)
Async XLA Ops:
  7.0 12.2 %copy-start.5 = (s32[128]{0:T(128)S(1)}, s32[128]{0:T(128)}, u32[]{:S(2)}) copy-start(s32[128]{0:T(128)} %param.19) | copy-start | bytes 1540
  19.3 13.0 %slice-start = ((s8[8388608]{0:T(1024)(128)(4,1)}), s8[4194304]{0:T(1024)(128)(4,1)S(1)}, s32[]{:S(2)}) async-start(s8[8388608]{0:T(1024)(128)(4,1)} %bitcast.26), calls=%async_computation | async-start | bytes 8388608
  24.7 7.6 %slice-start.1 = ((s8[8388608]{0:T(1024)(128)(4,1)}), s8[4194304]{0:T(1024)(128)(4,1)S(1)}, s32[]{:S(2)}) async-start(s8[8388608]{0:T(1024)(128)(4,1)} %bitcast.26), calls=%async_computation.1 | async-start | bytes 8388608
  24.7 7.6 %copy-start = (bf16[128,2048]{1,0:T(8,128)(2,1)S(1)}, bf16[128,2048]{1,0:T(8,128)(2,1)}, u32[]{:S(2)}) copy-start(bf16[128,2048]{1,0:T(8,128)(2,1)} %param.16) | copy-start | bytes 1572868
  32.3 1.6 %copy-start.3 = (bf16[2048]{0:T(1024)(128)(2,1)S(1)}, bf16[2048]{0:T(1024)(128)(2,1)}, u32[]{:S(2)}) copy-start(bf16[2048]{0:T(1024)(128)(2,1)} %param.23) | copy-start | bytes 12292
  32.3 3.3 %copy-start.2 = (s32[128,6]{0,1:T(8,128)S(1)}, s32[128,6]{0,1:T(8,128)}, u32[]{:S(2)}) copy-start(s32[128,6]{0,1:T(8,128)} %param.20) | copy-start | bytes 9220
  32.3 3.5 %copy-start.4 = (f32[128,6]{0,1:T(8,128)S(1)}, f32[128,6]{0,1:T(8,128)}, u32[]{:S(2)}) copy-start(f32[128,6]{0,1:T(8,128)} %param.21) | copy-start | bytes 9220
  33.8 0.8 copy-start.1

commit v2 on v1

--- a/solution.py
+++ b/solution.py
@@ -14,6 +14,9 @@
 NK = 4
 N1 = 4
 N2 = 6
+GS = 8
+NS = 3
+PC = 128
 PIECES = 3
 
 
@@ -23,29 +26,151 @@
     return (v * r * w.astype(F32)).astype(BF)
 
 
-def _attn(x, kk, vv, lens, ln1, wq, wo):
-    b, l, kvh, dh = kk.shape
-    hq = wq.shape[1] // dh
-    a = _rms(x, ln1)
-    q = jnp.dot(a, wq, preferred_element_type=F32).astype(BF).reshape(b, kvh, hq // kvh, dh)
-    s = jnp.einsum('bkgd,blkd->bkgl', q, kk, preferred_element_type=F32) * dh ** -0.5
-    valid = jnp.arange(l)[None, :] < lens[:, None]
-    s = jnp.where(valid[:, None, None, :], s, -jnp.inf)
-    p = jax.nn.softmax(s, axis=-1).astype(BF)
-    o = jnp.einsum('bkgl,blkd->bkgd', p, vv, preferred_element_type=F32).astype(BF)
-    attn = jnp.dot(o.reshape(b, hq * dh), wo, preferred_element_type=F32)
-    return (x.astype(F32) + attn).astype(BF)
-
-
-def _tables(topk, gates, n_exp, ndev, cap, ex_idx):
-    b = topk.shape[0]
-    hit = topk.T[None, :, :] == jnp.arange(n_exp, dtype=topk.dtype)[:, None, None]
-    chosen = hit.any(axis=1)
-    gate = jnp.where(hit, gates.T[None, :, :], 0.0).sum(axis=1)
-    tri = (jnp.arange(b)[:, None] < jnp.arange(b)[None, :]).astype(BF)
-    before = jnp.dot(chosen.astype(BF), tri, preferred_element_type=F32)
-    slot = jnp.where(chosen & (before < cap), before + (cap * ex_idx).astype(F32), -1.0)
-    return jnp.stack([slot.reshape(ndev, -1, b), gate.reshape(ndev, -1, b)], axis=1)
+def _attn_kernel(dims, lens_ref, x_ref, kv_k, kv_v, topk_ref, gates_ref, ln1_ref, ln2_ref, wq, wo,
+                 h_ref, u_ref, tab_ref, wqb, wob, kb, vb, qs, os, oall, sq, so, sk):
+    b, d, l, dh, nq, el, cap = dims
+    hd = nq * dh
+    qc = hd // 4
+    ng = b // GS
+    np_ = GS // 2
+
+    def cpq(n):
+        return pltpu.make_async_copy(wq.at[:, pl.ds(n * qc, qc)], wqb.at[n], sq.at[n])
+
+    def cpo(n):
+        return pltpu.make_async_copy(wo.at[:, pl.ds(n * qc, qc)], wob.at[n], so.at[n])
+
+    for n in range(4):
+        cpq(n).start()
+
+    def nch(s):
+        return (lens_ref[s] + PC - 1) // PC
+
+    def cpk(src, dst, g, i, c, which):
+        slot = g % NS
+        ps = pl.ds(pl.multiple_of(c * PC, PC), PC)
+        return pltpu.make_async_copy(
+            src.at[g * GS + i, ps, :], dst.at[slot, i // 2, ps, pl.ds((i % 2) * dh, dh)], sk.at[slot, which])
+
+    def fetch(g):
+        for i in range(GS):
+            def one(c, _, i=i):
+                cpk(kv_k, kb, g, i, c, 0).start()
+                cpk(kv_v, vb, g, i, c, 1).start()
+                return 0
+            lax.fori_loop(0, nch(g * GS + i), one, 0)
+
+    def fetched(g):
+        n = nch(g * GS)
+        for i in range(1, GS):
+            n = n + nch(g * GS + i)
+
+        def one(c, _):
+            cpk(kv_k, kb, g, 0, 0, 0).wait()
+            cpk(kv_v, vb, g, 0, 0, 1).wait()
+            return 0
+        lax.fori_loop(0, n, one, 0)
+
+    def clear(s, _):
+        for p in range(np_):
+            kb[s, p] = jnp.zeros((l, 2 * dh), BF)
+            vb[s, p] = jnp.zeros((l, 2 * dh), BF)
+        return 0
+    lax.fori_loop(0, NS, clear, 0)
+    for g in range(NS):
+        fetch(jnp.int32(g))
+    for n in range(4):
+        cpo(n).start()
+
+    n_exp = tab_ref.shape[0] * el
+    eidx = lax.broadcasted_iota(jnp.int32, (n_exp, b), 0)
+    hit = eidx < 0
+    gate = jnp.zeros((n_exp, b), F32)
+    for j in range(topk_ref.shape[0]):
+        m = topk_ref[j:j + 1, :] == eidx
+        hit = hit | m
+        gate = gate + jnp.where(m, gates_ref[j:j + 1, :], 0.0)
+    chosen = jnp.where(hit, 1.0, 0.0)
+    tri = jnp.where(lax.broadcasted_iota(jnp.int32, (b, b), 0) < lax.broadcasted_iota(jnp.int32, (b, b), 1), 1.0, 0.0)
+    before = jnp.dot(chosen.astype(BF), tri.astype(BF), preferred_element_type=F32)
+    off = (lax.axis_index('ex') * cap).astype(F32)
+    slot_ = jnp.where(hit & (before < cap), before + off, -1.0)
+    for e in range(tab_ref.shape[0]):
+        tab_ref[e, 0] = slot_[e * el:(e + 1) * el]
+        tab_ref[e, 1] = gate[e * el:(e + 1) * el]
+
+    a = _rms(x_ref[...], ln1_ref[...])
+    for n in range(4):
+        cpq(n).wait()
+        qn = jnp.dot(a, wqb[n], preferred_element_type=F32).astype(BF).astype(F32)
+        for i in range(qc // dh):
+            qs[:, n * (qc // dh) + i, :] = qn[:, i * dh:(i + 1) * dh]
+
+    pos = lax.broadcasted_iota(jnp.int32, (nq, l), 1)
+    zero = jnp.zeros((nq, dh), BF)
+
+    def step(g, _):
+        fetched(g)
+        slot = g % NS
+        for p in range(np_):
+            s0 = g * GS + 2 * p
+            q0 = jnp.concatenate([qs[s0].astype(BF), zero], axis=1)
+            q1 = jnp.concatenate([zero, qs[s0 + 1].astype(BF)], axis=1)
+            lhs = jnp.concatenate([q0, q1], axis=0)
+            s = lax.dot_general(lhs, kb[slot, p], (((1,), (1,)), ((), ())), preferred_element_type=F32) * dh ** -0.5
+            valid = jnp.concatenate([pos < lens_ref[s0], pos < lens_ref[s0 + 1]], axis=0)
+            s = jnp.where(valid, s, -jnp.inf)
+            e = jnp.exp(s - jnp.max(s, axis=-1, keepdims=True))
+            pr = (e * (1.0 / jnp.sum(e, axis=-1, keepdims=True))).astype(BF)
+            o = jnp.dot(pr, vb[slot, p], preferred_element_type=F32).astype(BF).astype(F32)
+            os[s0] = o[0:nq, 0:dh]
+            os[s0 + 1] = o[nq:2 * nq, dh:2 * dh]
+
+        @pl.when(g + NS < ng)
+        def _():
+            fetch(g + NS)
+        return 0
+
+    lax.fori_loop(0, ng, step, 0)
+    for i in range(nq):
+        oall[:, i * dh:(i + 1) * dh] = os[:, i, :].astype(BF)
+    for n in range(4):
+        cpo(n).wait()
+        cs = slice(n * qc, (n + 1) * qc)
+        h_ref[:, cs] = (x_ref[:, cs].astype(F32)
+                        + jnp.dot(oall[...], wob[n], preferred_element_type=F32)).astype(BF)
+    u_ref[...] = _rms(h_ref[...], ln2_ref[...])
+
+
+def _attention(x, kv_k, kv_v, lens, topk, gates, ln1, ln2, wq, wo, el, ndev, cap):
+    b, d = x.shape
+    _, l, kvh, dh = kv_k.shape
+    hd = wq.shape[1]
+    nq = hd // dh
+    vm = pl.BlockSpec(memory_space=pltpu.VMEM)
+    hb = pl.BlockSpec(memory_space=pltpu.HBM)
+    sm = pl.BlockSpec(memory_space=pltpu.SMEM)
+    dma = pltpu.SemaphoreType.DMA
+    return pl.pallas_call(
+        functools.partial(_attn_kernel, (b, d, l, dh, nq, el, cap)),
+        out_shape=(jax.ShapeDtypeStruct((b, d), BF), jax.ShapeDtypeStruct((b, d), BF),
+                   jax.ShapeDtypeStruct((ndev, 2, el, b), F32)),
+        in_specs=[sm, vm, hb, hb, vm, vm, vm, vm, hb, hb],
+        out_specs=(vm, vm, vm),
+        scratch_shapes=[
+            pltpu.VMEM((4, d, hd // 4), BF),
+            pltpu.VMEM((4, hd, d // 4), BF),
+            pltpu.VMEM((NS, GS // 2, l, 2 * dh), BF),
+            pltpu.VMEM((NS, GS // 2, l, 2 * dh), BF),
+            pltpu.VMEM((b, nq, dh), F32),
+            pltpu.VMEM((b, nq, dh), F32),
+            pltpu.VMEM((b, hd), BF),
+            dma((4,)), dma((4,)), dma((NS, 2)),
+        ],
+        compiler_params=pltpu.CompilerParams(vmem_limit_bytes=56 * 1024 * 1024),
+        name='attn',
+    )(lens, x, kv_k.reshape(b, l, dh), kv_v.reshape(b, l, dh), topk.T, gates.T,
+      ln1.reshape(1, d), ln2.reshape(1, d), wq, wo)
 
 
 def _moe_kernel(dims, u_ref, h_ref, tab_ref, w1, w3, w2, ws1, ws3, ws2, y_ref,
@@ -435,9 +560,7 @@
         b = x.shape[0]
         n_exp = w1.shape[0] * ndev
         cap = max(4, (2 * b * topk_idx.shape[1] + n_exp - 1) // n_exp)
-        tab = _tables(topk_idx, gates, n_exp, ndev, cap, lax.axis_index('ex'))
-        h = _attn(x, kv_k, kv_v, lens, ln1, wq, wo)
-        u = _rms(h, ln2)
+        h, u, tab = _attention(x, kv_k, kv_v, lens, topk_idx, gates, ln1, ln2, wq, wo, w1.shape[0], ndev, cap)
         return _moe(u, h, tab, w1, w3, w2, ws1, ws3, ws2, cap)
 
     return jax.shard_map(

time: 147 us -> 158 us (1.075)
  Pallas kernels: 108 us -> 153 us
  matrix products: 26.3 us -> 0 us
  other arithmetic: 9.1 us -> 0 us
  local copies, waits for them, and re-layouts: 2.8 us -> 4.45 us
    pallas_call x0 -> x1, Pallas kernels: none -> 44.6 us  [_attention(): pl.pallas_call(functools.partial(_attn_kernel, (b, d, l, dh, nq, el, cap)...]
    dot_general x5 -> x0, matrix products: 26.3 us -> none  [the longest x1 12.2 us: _attn(): jnp.einsum('bkgd,blkd->bkgl', q, kk, preferred_element_type=F32)]
    sub x1 -> x0, other arithmetic: 5.41 us -> none  [_attn(): p = jax.nn.softmax(s, axis=-1).astype(BF)]
    reshape x0 -> x2, local copies, waits for them, and re-layouts: none -> 2.57 us  [the longest x1 1.29 us: _attention(): ln2.reshape(1, d)]
    convert_element_type x3 -> x0, other arithmetic: 1.67 us -> none  [_rms(): return (v * r * w.astype(F32)).astype(BF)]
where the time goes in v2:
time: 158 us
  Pallas kernels  153 us (97%)
  local copies, waits for them, and re-layouts  4.45 us (3%)
    pallas_call x1, Pallas kernels, _moe(): pl.pallas_call(functools.partial(_moe_kernel, (b, d, ff, el, cap)), out_s...  109 us
    pallas_call x1, Pallas kernels, _attention(): pl.pallas_call(functools.partial(_attn_kernel, (b, d, l, dh, nq, el, cap)...  44.6 us

profile of v2, /device:TPU:0, one launch (start us, length us, event | category | flops | bytes accessed | tf_op | source)
XLA Modules:
  0.0 157.9 jit_solution(1594978829676989198)
XLA Ops:
  0.0 1.3 reshape.14.ln1_ref
  1.3 1.3 reshape.15.ln2_ref
  2.6 44.6 %attn.1 = (bf16[128,2048]{1,0:T(8,128)(2,1)}, bf16[128,2048]{1,0:T(8,128)(2,1)}, f32[8,2,8,128]{3,2,1,0:T(8,128)}) custom-call(s32[128]{0:T(128)} %lens_ref.1, bf16[128,2048]{1,0:T(8,128)(2,1)} %x_ref.1, bf16[128,512,128]{2,1,0:T(8,128)(2,1)} %bitcast.4, bf16[128,512,128]{2,1,0:T(8,128)(2,1)} %bitcast.5, s32[6,128]{1,0:T(8,128)} %bitcast.6, ...), custom_call_target="tpu_custom_call" | custom-call | tf_op jit(solution)/shard_map/attn/pallas_call | solution.py:154
  47.2 108.8 %moe.1 = bf16[128,2048]{1,0:T(8,128)(2,1)} custom-call(bf16[128,2048]{1,0:T(8,128)(2,1)} %get-tuple-element.8.u_ref, bf16[128,2048]{1,0:T(8,128)(2,1)} %get-tuple-element.9.h_ref, f32[8,2,8,128]{3,2,1,0:T(8,128)} %get-tuple-element.10.tab_ref, bf16[8,2048,1408]{2,1,0:T(8,128)(2,1)} %w1.1, bf16[8,2048,1408]{2,1,0:T(8,128)(2,1)} %w3.1, ...), custom_call_target="tpu_custom_call" | custom-call | tf_op jit(solution)/shard_map/moe/pallas_call | solution.py:519
  156.0 1.9 %copy.18 = bf16[128,2048]{1,0:T(8,128)(2,1)} copy(bf16[128,2048]{1,0:T(8,128)(2,1)} %moe.1) | data formatting | bytes 1048576

commit v3 on v2

--- a/solution.py
+++ b/solution.py
@@ -15,8 +15,8 @@
 N1 = 4
 N2 = 6
 GS = 8
-NS = 3
-PC = 128
+NS = 5
+SHORT = 64
 PIECES = 3
 
 
@@ -27,7 +27,7 @@
 
 
 def _attn_kernel(dims, lens_ref, x_ref, kv_k, kv_v, topk_ref, gates_ref, ln1_ref, ln2_ref, wq, wo,
-                 h_ref, u_ref, tab_ref, wqb, wob, kb, vb, qs, os, oall, sq, so, sk):
+                 h_ref, u_ref, tab_ref, wqb, wob, kb, vb, qs, os, oall, sb, pb, sq, so, sk):
     b, d, l, dh, nq, el, cap = dims
     hd = nq * dh
     qc = hd // 4
@@ -43,33 +43,28 @@
     for n in range(4):
         cpq(n).start()
 
-    def nch(s):
-        return (lens_ref[s] + PC - 1) // PC
-
-    def cpk(src, dst, g, i, c, which):
+    def fetch(g):
         slot = g % NS
-        ps = pl.ds(pl.multiple_of(c * PC, PC), PC)
-        return pltpu.make_async_copy(
-            src.at[g * GS + i, ps, :], dst.at[slot, i // 2, ps, pl.ds((i % 2) * dh, dh)], sk.at[slot, which])
-
-    def fetch(g):
         for i in range(GS):
-            def one(c, _, i=i):
-                cpk(kv_k, kb, g, i, c, 0).start()
-                cpk(kv_v, vb, g, i, c, 1).start()
-                return 0
-            lax.fori_loop(0, nch(g * GS + i), one, 0)
+            ls = pl.ds((i % 2) * dh, dh)
+            full = lens_ref[g * GS + i] > SHORT
+            for cond, n in ((full, l), (jnp.logical_not(full), SHORT)):
+                @pl.when(cond)
+                def _(i=i, n=n, ls=ls):
+                    for src, dst in ((kv_k, kb), (kv_v, vb)):
+                        pltpu.make_async_copy(
+                            src.at[g * GS + i, pl.ds(0, n), :], dst.at[slot, i // 2, pl.ds(0, n), ls],
+                            sk.at[slot]).start()
 
     def fetched(g):
-        n = nch(g * GS)
-        for i in range(1, GS):
-            n = n + nch(g * GS + i)
-
-        def one(c, _):
-            cpk(kv_k, kb, g, 0, 0, 0).wait()
-            cpk(kv_v, vb, g, 0, 0, 1).wait()
-            return 0
-        lax.fori_loop(0, n, one, 0)
+        slot = g % NS
+        for i in range(GS):
+            full = lens_ref[g * GS + i] > SHORT
+            for cond, n in ((full, l), (jnp.logical_not(full), SHORT)):
+                @pl.when(cond)
+                def _(n=n):
+                    blk = kb.at[slot, 0, pl.ds(0, n), :]
+                    pltpu.make_async_copy(blk, blk, sk.at[slot]).wait()
 
     def clear(s, _):
         for p in range(np_):
@@ -77,7 +72,7 @@
             vb[s, p] = jnp.zeros((l, 2 * dh), BF)
         return 0
     lax.fori_loop(0, NS, clear, 0)
-    for g in range(NS):
+    for g in range(NS - 2):
         fetch(jnp.int32(g))
     for n in range(4):
         cpo(n).start()
@@ -99,7 +94,7 @@
         tab_ref[e, 0] = slot_[e * el:(e + 1) * el]
         tab_ref[e, 1] = gate[e * el:(e + 1) * el]
 
-    a = _rms(x_ref[...], ln1_ref[...])
+    a = _rms(x_ref[...], ln1_ref[...].reshape(1, d))
     for n in range(4):
         cpq(n).wait()
         qn = jnp.dot(a, wqb[n], preferred_element_type=F32).astype(BF).astype(F32)
@@ -109,29 +104,54 @@
     pos = lax.broadcasted_iota(jnp.int32, (nq, l), 1)
     zero = jnp.zeros((nq, dh), BF)
 
-    def step(g, _):
-        fetched(g)
+    def scores(g):
         slot = g % NS
         for p in range(np_):
             s0 = g * GS + 2 * p
             q0 = jnp.concatenate([qs[s0].astype(BF), zero], axis=1)
             q1 = jnp.concatenate([zero, qs[s0 + 1].astype(BF)], axis=1)
             lhs = jnp.concatenate([q0, q1], axis=0)
-            s = lax.dot_general(lhs, kb[slot, p], (((1,), (1,)), ((), ())), preferred_element_type=F32) * dh ** -0.5
+            sb[p] = lax.dot_general(lhs, kb[slot, p], (((1,), (1,)), ((), ())), preferred_element_type=F32)
+
+    def softmax(g):
+        for p in range(np_):
+            s0 = g * GS + 2 * p
             valid = jnp.concatenate([pos < lens_ref[s0], pos < lens_ref[s0 + 1]], axis=0)
-            s = jnp.where(valid, s, -jnp.inf)
+            s = jnp.where(valid, sb[p] * dh ** -0.5, -jnp.inf)
             e = jnp.exp(s - jnp.max(s, axis=-1, keepdims=True))
-            pr = (e * (1.0 / jnp.sum(e, axis=-1, keepdims=True))).astype(BF)
-            o = jnp.dot(pr, vb[slot, p], preferred_element_type=F32).astype(BF).astype(F32)
+            pb[p] = (e * (1.0 / jnp.sum(e, axis=-1, keepdims=True))).astype(BF)
+
+    def values(g):
+        slot = g % NS
+        for p in range(np_):
+            s0 = g * GS + 2 * p
+            o = jnp.dot(pb[p], vb[slot, p], preferred_element_type=F32).astype(BF).astype(F32)
             os[s0] = o[0:nq, 0:dh]
             os[s0 + 1] = o[nq:2 * nq, dh:2 * dh]
 
-        @pl.when(g + NS < ng)
+    fetched(jnp.int32(0))
+    scores(jnp.int32(0))
+    fetch(jnp.int32(NS - 2))
+    fetched(jnp.int32(1))
+    softmax(jnp.int32(0))
+    scores(jnp.int32(1))
+    fetch(jnp.int32(NS - 1))
+
+    def step(g, _):
+        fetched(g)
+        values(g - 2)
+        softmax(g - 1)
+        scores(g)
+
+        @pl.when(g - 2 + NS < ng)
         def _():
-            fetch(g + NS)
+            fetch(g - 2 + NS)
         return 0
 
-    lax.fori_loop(0, ng, step, 0)
+    lax.fori_loop(2, ng, step, 0)
+    values(jnp.int32(ng - 2))
+    softmax(jnp.int32(ng - 1))
+    values(jnp.int32(ng - 1))
     for i in range(nq):
         oall[:, i * dh:(i + 1) * dh] = os[:, i, :].astype(BF)
     for n in range(4):
@@ -139,7 +159,7 @@
         cs = slice(n * qc, (n + 1) * qc)
         h_ref[:, cs] = (x_ref[:, cs].astype(F32)
                         + jnp.dot(oall[...], wob[n], preferred_element_type=F32)).astype(BF)
-    u_ref[...] = _rms(h_ref[...], ln2_ref[...])
+    u_ref[...] = _rms(h_ref[...], ln2_ref[...].reshape(1, d))
 
 
 def _attention(x, kv_k, kv_v, lens, topk, gates, ln1, ln2, wq, wo, el, ndev, cap):
@@ -165,12 +185,14 @@
             pltpu.VMEM((b, nq, dh), F32),
             pltpu.VMEM((b, nq, dh), F32),
             pltpu.VMEM((b, hd), BF),
-            dma((4,)), dma((4,)), dma((NS, 2)),
+            pltpu.VMEM((GS // 2, 2 * nq, l), F32),
+            pltpu.VMEM((GS // 2, 2 * nq, l), BF),
+            dma((4,)), dma((4,)), dma((NS,)),
         ],
         compiler_params=pltpu.CompilerParams(vmem_limit_bytes=56 * 1024 * 1024),
         name='attn',
     )(lens, x, kv_k.reshape(b, l, dh), kv_v.reshape(b, l, dh), topk.T, gates.T,
-      ln1.reshape(1, d), ln2.reshape(1, d), wq, wo)
+      ln1, ln2, wq, wo)
 
 
 def _moe_kernel(dims, u_ref, h_ref, tab_ref, w1, w3, w2, ws1, ws3, ws2, y_ref,

time: 158 us -> 132 us (0.84)
  Pallas kernels: 153 us -> 130 us
  local copies, waits for them, and re-layouts: 4.45 us -> 1.88 us
    pallas_call x1, Pallas kernels: 44.6 us -> 21.2 us  [_attention(): pl.pallas_call(functools.partial(_attn_kernel, (b, d, l, dh, nq, el, cap)...]
    reshape x2 -> x0, local copies, waits for them, and re-layouts: 2.57 us -> none  [the longest x1 1.29 us: _attention(): ln2.reshape(1, d)]
where the time goes in v3:
time: 132 us
  Pallas kernels  130 us (98%)
  local copies, waits for them, and re-layouts  1.88 us (1%)
    pallas_call x1, Pallas kernels, _moe(): pl.pallas_call(functools.partial(_moe_kernel, (b, d, ff, el, cap)), out_s...  108 us
    pallas_call x1, Pallas kernels, _attention(): pl.pallas_call(functools.partial(_attn_kernel, (b, d, l, dh, nq, el, cap)...  21.2 us

profile of v3, /device:TPU:0, one launch (start us, length us, event | category | flops | bytes accessed | tf_op | source)
XLA Modules:
  0.0 131.5 jit_solution(9295692189902223038)
XLA Ops:
  0.0 21.2 %attn.1 = (bf16[128,2048]{1,0:T(8,128)(2,1)}, bf16[128,2048]{1,0:T(8,128)(2,1)}, f32[8,2,8,128]{3,2,1,0:T(8,128)}) custom-call(s32[128]{0:T(128)} %lens_ref.1, bf16[128,2048]{1,0:T(8,128)(2,1)} %x_ref.1, bf16[128,512,128]{2,1,0:T(8,128)(2,1)} %bitcast.4, bf16[128,512,128]{2,1,0:T(8,128)(2,1)} %bitcast.5, s32[6,128]{1,0:T(8,128)} %bitcast.6, ...), custom_call_target="tpu_custom_call" | custom-call | tf_op jit(solution)/shard_map/attn/pallas_call | solution.py:174
  21.2 108.4 %moe.1 = bf16[128,2048]{1,0:T(8,128)(2,1)} custom-call(bf16[128,2048]{1,0:T(8,128)(2,1)} %get-tuple-element.8.u_ref, bf16[128,2048]{1,0:T(8,128)(2,1)} %get-tuple-element.9.h_ref, f32[8,2,8,128]{3,2,1,0:T(8,128)} %get-tuple-element.10.tab_ref, bf16[8,2048,1408]{2,1,0:T(8,128)(2,1)} %w1.1, bf16[8,2048,1408]{2,1,0:T(8,128)(2,1)} %w3.1, ...), custom_call_target="tpu_custom_call" | custom-call | tf_op jit(solution)/shard_map/moe/pallas_call | solution.py:541
  129.6 1.9 %copy.18 = bf16[128,2048]{1,0:T(8,128)(2,1)} copy(bf16[128,2048]{1,0:T(8,128)(2,1)} %moe.1) | data formatting | bytes 1048576

commit v4 on v3

--- a/solution.py
+++ b/solution.py
@@ -338,6 +338,9 @@
     for n, nw in nts:
         zs[:, n:n + nw] = silu_mul(acc[0, 0:b, n:n + nw], acc[1, 0:b, n:n + nw])
 
+    forward(0)
+    direct(2)
+
     for o in range(1, 8):
         src = (me + 8 - o) % 8
         pltpu.make_async_remote_copy(
@@ -364,9 +367,11 @@
 
     lax.fori_loop(0, 4, build, 0)
 
-    forward(0)
-    direct(2)
+    forward(1)
+    direct(3)
     forward_diag(0)
+    events = {(0, 2): lambda: forward(2), (0, 4): lambda: forward_diag(1), (0, 6): lambda: forward(3),
+              (1, 2): lambda: forward_diag(2), (1, 4): lambda: forward_diag(3)}
 
     for k in range(NK):
         arrived(k)
@@ -380,6 +385,9 @@
         lax.fori_loop(0, 4, pick, 0)
 
         def zstep(e, _, k=k):
+            for (ke, at), event in events.items():
+                if ke == k:
+                    pl.when(e == at)(event)
             s = NK + k * el + e
             wait13(s)
             slot = s % N1
@@ -408,23 +416,17 @@
                     start2(nxt - n13)
             return 0
 
-        half = el // 2
-        lax.fori_loop(0, half, zstep, 0)
-        if k + 1 < NK:
-            forward(k + 1)
-            if k + 3 < NK:
-                direct(k + 3)
-        lax.fori_loop(half, el, zstep, 0)
-        if k + 1 < NK:
-            forward_diag(k + 1)
+        lax.fori_loop(0, el, zstep, 0)
     for j in range(N1, N2):
         start2(jnp.int32(j))
 
-    def part(c, e, chip):
-        return acc.at[c // 2, pl.ds(pl.multiple_of((e * 4 + chip) * b, b), b), pl.ds((c % 2) * cw, cw)]
-
-    def nbr(c):
-        return (xn, xdev, yn, ydev) if c % 2 == 0 else (yn, ydev, xn, xdev)
+    hw = cw // 2
+
+    def part(c, e, chip, j=None):
+        cols = pl.ds((c % 2) * cw, cw) if j is None else pl.ds((c % 2) * cw + j * hw, hw)
+        return acc.at[c // 2, pl.ds(pl.multiple_of((e * 4 + chip) * b, b), b), cols]
+
+    order = ((xn, xdev, yn, ydev), (yn, ydev, xn, xdev))
 
     def dcopy(c):
         src = acc.at[c // 2, pl.ds(pl.multiple_of(ox * 4 * b, 4 * b), 4 * b), pl.ds((c % 2) * cw, cw)]
@@ -432,42 +434,50 @@
             src_ref=src, dst_ref=d2d.at[c], send_sem=dsend.at[c], recv_sem=drecv.at[c],
             device_id=partner, device_id_type=MESH)
 
-    def pcopy(c, i):
-        n1, dev1, n2_, dev2 = nbr(c)
+    def pcopy(c, j, i):
+        first, dev, _, _ = order[j]
         return pltpu.make_async_remote_copy(
-            src_ref=part(c, ex, n1 if i == 0 else dg), dst_ref=rx1.at[c, i], send_sem=psend.at[c, i],
-            recv_sem=precv.at[c, i], device_id=dev1, device_id_type=MESH)
-
-    def qcopy(c):
-        n1, dev1, n2_, dev2 = nbr(c)
+            src_ref=part(c, ex, first if i == 0 else dg, j), dst_ref=rx1.at[c, j, i], send_sem=psend.at[c, j, i],
+            recv_sem=precv.at[c, j, i], device_id=dev, device_id_type=MESH)
+
+    def qcopy(c, j):
+        _, _, second, dev = order[j]
         return pltpu.make_async_remote_copy(
-            src_ref=part(c, ex, n2_), dst_ref=rx2.at[c], send_sem=qsend.at[c], recv_sem=qrecv.at[c],
-            device_id=dev2, device_id_type=MESH)
-
-    def step_a(c):
-        def down(e, _):
-            j = c * (el + 1) + e
-            wait2(j)
-            r = jnp.dot(z[e], r2[j % N2], preferred_element_type=F32).astype(BF)
-            for q in range(4):
-                outb[q, pl.ds(pl.multiple_of(e * pair, pair), pair), :] = r[q * pair:(q + 1) * pair, :]
-
-            @pl.when(j + N2 < n2)
-            def _():
-                start2(j + N2)
+            src_ref=part(c, ex, second, j), dst_ref=rx2.at[c, j], send_sem=qsend.at[c, j], recv_sem=qrecv.at[c, j],
+            device_id=dev, device_id_type=MESH)
+
+    def step_a(c, events):
+        def down(t, _):
+            for at, event in events:
+                pl.when(t == at)(event)
+            for i in range(2):
+                e = 2 * t + i
+                j = c * (el + 1) + e
+                wait2(j)
+                r = jnp.dot(z[e], r2[j % N2], preferred_element_type=F32).astype(BF)
+                for q in range(4):
+                    outb[q, pl.ds(pl.multiple_of(e * pair, pair), pair), :] = r[q * pair:(q + 1) * pair, :]
+            for i in range(2):
+                j = c * (el + 1) + 2 * t + i
+
+                @pl.when(j + N2 < n2)
+                def _(j=j):
+                    start2(j + N2)
             return 0
 
-        lax.fori_loop(0, el, down, 0)
-
-        def comb(q, _):
-            p = jnp.dot(wgt[0, q], outb[q], preferred_element_type=F32)
-            for i in range(1, PIECES):
-                p = p + jnp.dot(wgt[i, q], outb[q], preferred_element_type=F32)
-            part(c, 0, q)[...] = p[0:b]
-            part(c, 1, q)[...] = p[b:2 * b]
+        lax.fori_loop(0, el // 2, down, 0)
+
+        def comb(t, _):
+            for i in range(2):
+                q = 2 * t + i
+                p = jnp.dot(wgt[0, q], outb[q], preferred_element_type=F32)
+                for n in range(1, PIECES):
+                    p = p + jnp.dot(wgt[n, q], outb[q], preferred_element_type=F32)
+                part(c, 0, q)[...] = p[0:b]
+                part(c, 1, q)[...] = p[b:2 * b]
             return 0
 
-        lax.fori_loop(0, 4, comb, 0)
+        lax.fori_loop(0, 2, comb, 0)
         dcopy(c).start()
         j = c * (el + 1) + el
         wait2(jnp.int32(j))
@@ -483,36 +493,33 @@
             return 0
 
         lax.fori_loop(0, 4, add, 0)
-        pcopy(c, 1).start()
-        pcopy(c, 0).start()
+        for i in (1, 0):
+            for j in range(2):
+                pcopy(c, j, i).start()
 
     def step_c(c):
-        n1, dev1, n2_, dev2 = nbr(c)
-        pcopy(c, 1).wait_recv()
-        pcopy(c, 1).wait_send()
-        part(c, ex, n2_)[...] = part(c, ex, n2_)[...] + rx1[c, 1]
-        qcopy(c).start()
+        for j in range(2):
+            pcopy(c, j, 1).wait_recv()
+            second = order[j][2]
+            part(c, ex, second, j)[...] = part(c, ex, second, j)[...] + rx1[c, j, 1]
+            qcopy(c, j).start()
 
     def step_d(c):
-        pcopy(c, 0).wait_recv()
-        qcopy(c).wait_recv()
-        cs = slice(c * cw, (c + 1) * cw)
-        t = part(c, ex, ey)[...] + rx1[c, 0] + rx2[c]
-        y_ref[:, cs] = (h_ref[:, cs].astype(F32) + sh[:, cs].astype(F32) + t).astype(BF)
-
-    step_a(0)
-    step_a(1)
-    step_b(0)
-    step_b(1)
-    step_a(2)
-    step_c(0)
-    step_c(1)
-    step_a(3)
-    step_b(2)
+        for j in range(2):
+            pcopy(c, j, 0).wait_recv()
+            qcopy(c, j).wait_recv()
+            cs = slice(c * cw + j * hw, c * cw + (j + 1) * hw)
+            t = part(c, ex, ey, j)[...] + rx1[c, j, 0] + rx2[c, j]
+            y_ref[:, cs] = (h_ref[:, cs].astype(F32) + sh[:, cs].astype(F32) + t).astype(BF)
+
+    step_a(0, ())
+    step_a(1, ((2, lambda: step_b(0)),))
+    step_a(2, ((1, lambda: step_c(0)), (2, lambda: step_b(1))))
+    step_a(3, ((2, lambda: step_b(2)), (3, lambda: step_c(1))))
     step_b(3)
+    step_c(2)
     step_d(0)
     step_d(1)
-    step_c(2)
     step_c(3)
     step_d(2)
     step_d(3)
@@ -524,8 +531,10 @@
             ucopy(k, i, uown(k), ey, ex, 0, partner).wait_send()
     for c in range(NK):
         dcopy(c).wait_send()
-        pcopy(c, 0).wait_send()
-        qcopy(c).wait_send()
+        for j in range(2):
+            pcopy(c, j, 0).wait_send()
+            pcopy(c, j, 1).wait_send()
+            qcopy(c, j).wait_send()
 
 
 def _moe(u, h, tab, w1, w3, w2, ws1, ws3, ws2, cap):
@@ -555,16 +564,16 @@
             pltpu.VMEM((b, d), BF),
             pltpu.VMEM((4, el * pair, cw), BF),
             pltpu.VMEM((NK, 4 * b, cw), F32),
-            pltpu.VMEM((NK, 2, b, cw), F32),
-            pltpu.VMEM((NK, b, cw), F32),
+            pltpu.VMEM((NK, 2, 2, b, cw // 2), F32),
+            pltpu.VMEM((NK, 2, b, cw // 2), F32),
             pltpu.VMEM((N1, 2, cw, ff), BF),
             pltpu.VMEM((N2, ff, cw), BF),
             dma((N1, 2)), dma((N2,)),
             dma((7,)), dma((7,)),
             dma((NK, 7)), dma((NK, 7)), dma((NK,)),
             dma((NK,)), dma((NK,)),
+            dma((NK, 2, 2)), dma((NK, 2, 2)),
             dma((NK, 2)), dma((NK, 2)),
-            dma((NK,)), dma((NK,)),
         ],
         compiler_params=pltpu.CompilerParams(
             collective_id=0, has_side_effects=True, vmem_limit_bytes=67043328),

time: 132 us -> 119 us (0.902)
  Pallas kernels: 130 us -> 116 us
    pallas_call x1, Pallas kernels: 108 us -> 94.5 us  [_moe(): pl.pallas_call(functools.partial(_moe_kernel, (b, d, ff, el, cap)), out_s...]
where the time goes in v4:
time: 119 us; the launch traced here: 118 us
  Pallas kernels  116 us (97%)
  local copies, waits for them, and re-layouts  1.88 us (2%)
    pallas_call x1, Pallas kernels, _moe(): pl.pallas_call(functools.partial(_moe_kernel, (b, d, ff, el, cap)), out_s...  94.5 us
    pallas_call x1, Pallas kernels, _attention(): pl.pallas_call(functools.partial(_attn_kernel, (b, d, l, dh, nq, el, cap)...  21.5 us

profile of v4, /device:TPU:0, one launch (start us, length us, event | category | flops | bytes accessed | tf_op | source)
XLA Modules:
  0.0 117.9 jit_solution(14546184579615480640)
XLA Ops:
  0.0 21.5 %attn.1 = (bf16[128,2048]{1,0:T(8,128)(2,1)}, bf16[128,2048]{1,0:T(8,128)(2,1)}, f32[8,2,8,128]{3,2,1,0:T(8,128)}) custom-call(s32[128]{0:T(128)} %lens_ref.1, bf16[128,2048]{1,0:T(8,128)(2,1)} %x_ref.1, bf16[128,512,128]{2,1,0:T(8,128)(2,1)} %bitcast.4, bf16[128,512,128]{2,1,0:T(8,128)(2,1)} %bitcast.5, s32[6,128]{1,0:T(8,128)} %bitcast.6, ...), custom_call_target="tpu_custom_call" | custom-call | tf_op jit(solution)/shard_map/attn/pallas_call | solution.py:174
  21.5 94.5 %moe.1 = bf16[128,2048]{1,0:T(8,128)(2,1)} custom-call(bf16[128,2048]{1,0:T(8,128)(2,1)} %get-tuple-element.8.u_ref, bf16[128,2048]{1,0:T(8,128)(2,1)} %get-tuple-element.9.h_ref, f32[8,2,8,128]{3,2,1,0:T(8,128)} %get-tuple-element.10.tab_ref, bf16[8,2048,1408]{2,1,0:T(8,128)(2,1)} %w1.1, bf16[8,2048,1408]{2,1,0:T(8,128)(2,1)} %w3.1, ...), custom_call_target="tpu_custom_call" | custom-call | tf_op jit(solution)/shard_map/moe/pallas_call | solution.py:550
  116.0 1.9 %copy.18 = bf16[128,2048]{1,0:T(8,128)(2,1)} copy(bf16[128,2048]{1,0:T(8,128)(2,1)} %moe.1) | data formatting | bytes 1048576

commit v5 on v4

--- a/solution.py
+++ b/solution.py
@@ -14,8 +14,8 @@
 NK = 4
 N1 = 4
 N2 = 6
-GS = 8
-NS = 5
+GS = 16
+NS = 4
 SHORT = 64
 PIECES = 3
 
@@ -46,25 +46,27 @@
     def fetch(g):
         slot = g % NS
         for i in range(GS):
-            ls = pl.ds((i % 2) * dh, dh)
-            full = lens_ref[g * GS + i] > SHORT
-            for cond, n in ((full, l), (jnp.logical_not(full), SHORT)):
-                @pl.when(cond)
-                def _(i=i, n=n, ls=ls):
-                    for src, dst in ((kv_k, kb), (kv_v, vb)):
-                        pltpu.make_async_copy(
-                            src.at[g * GS + i, pl.ds(0, n), :], dst.at[slot, i // 2, pl.ds(0, n), ls],
-                            sk.at[slot]).start()
+            def copy(n, i=i):
+                for src, dst in ((kv_k, kb), (kv_v, vb)):
+                    pltpu.make_async_copy(
+                        src.at[g * GS + i, pl.ds(0, n), :],
+                        dst.at[slot, i // 2, pl.ds(0, n), pl.ds((i % 2) * dh, dh)], sk.at[slot]).start()
+
+            lax.cond(lens_ref[g * GS + i] > SHORT, lambda: copy(l), lambda: copy(SHORT))
 
     def fetched(g):
         slot = g % NS
+        full = jnp.int32(0)
         for i in range(GS):
-            full = lens_ref[g * GS + i] > SHORT
-            for cond, n in ((full, l), (jnp.logical_not(full), SHORT)):
-                @pl.when(cond)
-                def _(n=n):
-                    blk = kb.at[slot, 0, pl.ds(0, n), :]
-                    pltpu.make_async_copy(blk, blk, sk.at[slot]).wait()
+            full = full + (lens_ref[g * GS + i] > SHORT).astype(jnp.int32)
+
+        def wait(n):
+            blk = kb.at[slot, 0, pl.ds(0, n), :]
+            pltpu.make_async_copy(blk, blk, sk.at[slot]).wait()
+            return 0
+
+        lax.fori_loop(0, full, lambda i, _: wait(l), 0)
+        lax.fori_loop(full, GS, lambda i, _: wait(SHORT), 0)
 
     def clear(s, _):
         for p in range(np_):
@@ -260,6 +262,8 @@
 
     for s in range(N1):
         start13(jnp.int32(s))
+    for j in range(N2):
+        start2(jnp.int32(j))
 
     barrier = pltpu.get_barrier_semaphore()
     for o in range(1, 8):
@@ -372,6 +376,11 @@
     forward_diag(0)
     events = {(0, 2): lambda: forward(2), (0, 4): lambda: forward_diag(1), (0, 6): lambda: forward(3),
               (1, 2): lambda: forward_diag(2), (1, 4): lambda: forward_diag(3)}
+
+    def down_one(j, e):
+        r = jnp.dot(z[e], r2[j % N2], preferred_element_type=F32).astype(BF)
+        for q in range(4):
+            outb[q, pl.ds(pl.multiple_of(e * pair, pair), pair), :] = r[q * pair:(q + 1) * pair, :]
 
     for k in range(NK):
         arrived(k)
@@ -411,14 +420,12 @@
                 start13(nxt)
 
             if k == NK - 1:
-                @pl.when(nxt >= n13)
-                def _():
-                    start2(nxt - n13)
+                wait2(e)
+                down_one(e, e)
+                start2(e + N2)
             return 0
 
         lax.fori_loop(0, el, zstep, 0)
-    for j in range(N1, N2):
-        start2(jnp.int32(j))
 
     hw = cw // 2
 
@@ -428,11 +435,12 @@
 
     order = ((xn, xdev, yn, ydev), (yn, ydev, xn, xdev))
 
-    def dcopy(c):
-        src = acc.at[c // 2, pl.ds(pl.multiple_of(ox * 4 * b, 4 * b), 4 * b), pl.ds((c % 2) * cw, cw)]
+    def dcopy(c, t):
+        rs = pl.ds(pl.multiple_of((ox * 4 + 2 * t) * b, b), 2 * b)
         return pltpu.make_async_remote_copy(
-            src_ref=src, dst_ref=d2d.at[c], send_sem=dsend.at[c], recv_sem=drecv.at[c],
-            device_id=partner, device_id_type=MESH)
+            src_ref=acc.at[c // 2, rs, pl.ds((c % 2) * cw, cw)],
+            dst_ref=d2d.at[c, pl.ds(pl.multiple_of(2 * t * b, b), 2 * b)],
+            send_sem=dsend.at[c, t], recv_sem=drecv.at[c, t], device_id=partner, device_id_type=MESH)
 
     def pcopy(c, j, i):
         first, dev, _, _ = order[j]
@@ -451,12 +459,9 @@
             for at, event in events:
                 pl.when(t == at)(event)
             for i in range(2):
-                e = 2 * t + i
-                j = c * (el + 1) + e
-                wait2(j)
-                r = jnp.dot(z[e], r2[j % N2], preferred_element_type=F32).astype(BF)
-                for q in range(4):
-                    outb[q, pl.ds(pl.multiple_of(e * pair, pair), pair), :] = r[q * pair:(q + 1) * pair, :]
+                wait2(c * (el + 1) + 2 * t + i)
+            for i in range(2):
+                down_one(c * (el + 1) + 2 * t + i, 2 * t + i)
             for i in range(2):
                 j = c * (el + 1) + 2 * t + i
 
@@ -465,7 +470,8 @@
                     start2(j + N2)
             return 0
 
-        lax.fori_loop(0, el // 2, down, 0)
+        if c > 0:
+            lax.fori_loop(0, el // 2, down, 0)
 
         def comb(t, _):
             for i in range(2):
@@ -475,10 +481,10 @@
                     p = p + jnp.dot(wgt[n, q], outb[q], preferred_element_type=F32)
                 part(c, 0, q)[...] = p[0:b]
                 part(c, 1, q)[...] = p[b:2 * b]
+            dcopy(c, t).start()
             return 0
 
         lax.fori_loop(0, 2, comb, 0)
-        dcopy(c).start()
         j = c * (el + 1) + el
         wait2(jnp.int32(j))
         sh[:, c * cw:(c + 1) * cw] = jnp.dot(zs[...], r2[j % N2], preferred_element_type=F32).astype(BF)
@@ -486,7 +492,8 @@
             start2(jnp.int32(j + N2))
 
     def step_b(c):
-        dcopy(c).wait_recv()
+        dcopy(c, 0).wait_recv()
+        dcopy(c, 1).wait_recv()
 
         def add(q, _):
             part(c, ex, q)[...] = part(c, ex, q)[...] + d2d[c, pl.ds(pl.multiple_of(q * b, b), b), :]
@@ -513,9 +520,9 @@
             y_ref[:, cs] = (h_ref[:, cs].astype(F32) + sh[:, cs].astype(F32) + t).astype(BF)
 
     step_a(0, ())
-    step_a(1, ((2, lambda: step_b(0)),))
-    step_a(2, ((1, lambda: step_c(0)), (2, lambda: step_b(1))))
-    step_a(3, ((2, lambda: step_b(2)), (3, lambda: step_c(1))))
+    step_a(1, ((1, lambda: step_b(0)),))
+    step_a(2, ((0, lambda: step_c(0)), (1, lambda: step_b(1))))
+    step_a(3, ((0, lambda: step_c(1)), (1, lambda: step_b(2))))
     step_b(3)
     step_c(2)
     step_d(0)
@@ -530,7 +537,8 @@
         for i in range(7):
             ucopy(k, i, uown(k), ey, ex, 0, partner).wait_send()
     for c in range(NK):
-        dcopy(c).wait_send()
+        dcopy(c, 0).wait_send()
+        dcopy(c, 1).wait_send()
         for j in range(2):
             pcopy(c, j, 0).wait_send()
             pcopy(c, j, 1).wait_send()
@@ -571,7 +579,7 @@
             dma((N1, 2)), dma((N2,)),
             dma((7,)), dma((7,)),
             dma((NK, 7)), dma((NK, 7)), dma((NK,)),
-            dma((NK,)), dma((NK,)),
+            dma((NK, 2)), dma((NK, 2)),
             dma((NK, 2, 2)), dma((NK, 2, 2)),
             dma((NK, 2)), dma((NK, 2)),
         ],

time: 119 us -> 117 us (0.983)
  Pallas kernels: 116 us -> 114 us
where the time goes in v5:
time: 117 us; the launch traced here: 116 us
  Pallas kernels  114 us (97%)
  local copies, waits for them, and re-layouts  1.88 us (2%)
    pallas_call x1, Pallas kernels, _moe(): pl.pallas_call(functools.partial(_moe_kernel, (b, d, ff, el, cap)), out_s...  93.6 us
    pallas_call x1, Pallas kernels, _attention(): pl.pallas_call(functools.partial(_attn_kernel, (b, d, l, dh, nq, el, cap)...  20.9 us

profile of v5, /device:TPU:0, one launch (start us, length us, event | category | flops | bytes accessed | tf_op | source)
XLA Modules:
  0.0 116.4 jit_solution(7495162547439669776)
XLA Ops:
  0.0 20.9 %attn.1 = (bf16[128,2048]{1,0:T(8,128)(2,1)}, bf16[128,2048]{1,0:T(8,128)(2,1)}, f32[8,2,8,128]{3,2,1,0:T(8,128)}) custom-call(s32[128]{0:T(128)} %lens_ref.1, bf16[128,2048]{1,0:T(8,128)(2,1)} %x_ref.1, bf16[128,512,128]{2,1,0:T(8,128)(2,1)} %bitcast.4, bf16[128,512,128]{2,1,0:T(8,128)(2,1)} %bitcast.5, s32[6,128]{1,0:T(8,128)} %bitcast.6, ...), custom_call_target="tpu_custom_call" | custom-call | tf_op jit(solution)/shard_map/attn/pallas_call | solution.py:176
  20.9 93.6 %moe.1 = bf16[128,2048]{1,0:T(8,128)(2,1)} custom-call(bf16[128,2048]{1,0:T(8,128)(2,1)} %get-tuple-element.8.u_ref, bf16[128,2048]{1,0:T(8,128)(2,1)} %get-tuple-element.9.h_ref, f32[8,2,8,128]{3,2,1,0:T(8,128)} %get-tuple-element.10.tab_ref, bf16[8,2048,1408]{2,1,0:T(8,128)(2,1)} %w1.1, bf16[8,2048,1408]{2,1,0:T(8,128)(2,1)} %w3.1, ...), custom_call_target="tpu_custom_call" | custom-call | tf_op jit(solution)/shard_map/moe/pallas_call | solution.py:558
  114.5 1.9 %copy.18 = bf16[128,2048]{1,0:T(8,128)(2,1)} copy(bf16[128,2048]{1,0:T(8,128)(2,1)} %moe.1) | data formatting | bytes 1048576
